TPU v7x, 32 devices: a whole 2x2x4 slice. The times are simulated.
32 devices in a mesh: spec: 4 (over y, core), lat: 8 (over z, x).
Axes of the slice: x: 2, y: 2, z: 4, core: 2. Of those that a mesh axis runs over, the one named last changes fastest.
Arguments:
- concentration: float32 [256, 32, 512], P('spec', 'lat'), may hold values from 0.05 to 2
- courant: float32 [32, 512], P('lat'), may hold values from -0.9 to 0.9
- rate_const: float32 [1024], replicated, may hold values from 0.005 to 0.08
- reactants: int32 [1024, 2], replicated, may hold values from 0 to 255
- products: int32 [1024, 2], replicated, may hold values from 0 to 255
- daylit: int32 [32], replicated, may hold values from 0 to 1, as said below
- block_slot: int32 [32], replicated, may hold values from 0 to 31, as said below
Outputs:
- states: float32 [256, 32, 512], P(None, 'lat', 'spec')
Inputs may be any that keep to these rules, and one draw needn't show every extreme that they name: block_slot is a permutation of the 32 rows. Grouping rows into groups of 4 in order, every row's slot lies in its own group or in the group just before or after it, and every group moves exactly one row into each neighbouring group that exists. Of the 4 slots of every group, exactly 2 are taken by rows with daylit equal to 1.
All inputs are finite; a program needn't handle non-finite values.
Results may differ from a plain program's by a relative error of at most 0.0003.
Values sent between devices are 32-bit elements; how exact they have to be, the bound alone decides.
No kernel may reach another device: no remote copies, remote signals or barrier semaphores. Data moves between devices by JAX's collectives and lax.ppermute only.
A program may use at most 64 MiB of HBM per device.

v0:
```python
import jax
import jax.numpy as jnp
from jax import lax
from jax.sharding import PartitionSpec as P

ADV_STEPS = 2
SUBSTEPS = 2


def padded_2(block, sides, width):
    for axis, dim in sides:
        count = lax.axis_size(axis)
        forward = [(i, i + 1) for i in range(count - 1)]
        backward = [(target, source) for source, target in forward]
        low = lax.ppermute(
            lax.slice_in_dim(block, block.shape[dim] - width, None, axis=dim), axis, forward
        )
        high = lax.ppermute(lax.slice_in_dim(block, 0, width, axis=dim), axis, backward)
        block = jnp.concatenate([low, block, high], axis=dim)
    return block


def passed_along(value, axis, by):
    peers = lax.axis_size(axis)
    pairs = [(i, i + by) for i in range(peers) if 0 <= i + by < peers]
    return lax.ppermute(value, axis, pairs)


def minmod(left, right):
    return 0.5 * (jnp.sign(left) + jnp.sign(right)) * jnp.minimum(jnp.abs(left), jnp.abs(right))


def sweep_rows(values, flow_rows, first_row, lat_total):
    row_count = values.shape[1]
    steps_up = values[:, 1:] - values[:, :-1]
    slopes = minmod(steps_up[:, 1:], steps_up[:, :-1])
    face_index = first_row + 2 + jnp.arange(row_count - 3, dtype=jnp.int32)
    inside = ((face_index >= 1) & (face_index <= lat_total - 1))[:, None]
    numbers = jnp.where(inside, flow_rows[2 : row_count - 1], 0.0)
    forward = jnp.maximum(numbers, 0.0) * (
        values[:, 1 : row_count - 2] + 0.5 * (1.0 - numbers) * slopes[:, 0 : row_count - 3]
    )
    backward = jnp.minimum(numbers, 0.0) * (
        values[:, 2 : row_count - 1] - 0.5 * (1.0 + numbers) * slopes[:, 1 : row_count - 2]
    )
    fluxes = forward + backward
    return values[:, 2 : row_count - 2] - (fluxes[:, 1:] - fluxes[:, :-1])


def react_cells(conc, reactants, products, rate_const):
    species_count = conc.shape[0]
    for repeat in range(SUBSTEPS):
        first_conc = jnp.take(conc, reactants[:, 0], axis=0)
        second_conc = jnp.take(conc, reactants[:, 1], axis=0)
        encounter = first_conc * second_conc
        rates = rate_const[:, None] * encounter / (1.0 + jnp.abs(encounter))
        gained = jax.ops.segment_sum(rates, products[:, 0], num_segments=species_count)
        gained = gained + jax.ops.segment_sum(rates, products[:, 1], num_segments=species_count)
        lost = jax.ops.segment_sum(rates, reactants[:, 0], num_segments=species_count)
        lost = lost + jax.ops.segment_sum(rates, reactants[:, 1], num_segments=species_count)
        conc = conc + (gained - lost)
    return conc


def on_device(concentration, courant, rate_const, reactants, products, daylit, block_slot):
    lat_rows = concentration.shape[1]
    lat_index = lax.axis_index("lat")
    lat_total = lat_rows * lax.axis_size("lat")
    base_row = lat_index * lat_rows
    values = concentration
    for repeat in range(ADV_STEPS):
        stacked = jnp.concatenate([values, courant[None]], 0)
        padded = padded_2(stacked, (("lat", 1),), 2)
        values = sweep_rows(padded[:-1], padded[-1], base_row - 2, lat_total)
    cells = lax.all_to_all(values, "spec", split_axis=2, concat_axis=0, tiled=True)
    row_ids = jnp.arange(lat_rows, dtype=jnp.int32)
    my_slots = lax.dynamic_slice_in_dim(block_slot, base_row, lat_rows)
    my_target = my_slots // lat_rows
    received = []
    for direction in (1, -1):
        chosen = jnp.sum(jnp.where(my_target == lat_index + direction, row_ids, 0))
        outgoing = lax.dynamic_index_in_dim(cells, chosen, 1, keepdims=True)
        received.append(passed_along(outgoing, "lat", direction))
    candidates = jnp.concatenate([cells] + received, 1)
    own_slots = base_row + row_ids
    matches = (block_slot[None, :] == own_slots[:, None]).astype(jnp.int32)
    all_rows = jnp.arange(block_slot.shape[0], dtype=jnp.int32)
    source = jnp.sum(matches * all_rows[None, :], axis=1)
    day_flag = jnp.sum(matches * daylit[None, :], axis=1)
    source_band = source // lat_rows
    pick_index = jnp.where(
        source_band == lat_index,
        source - base_row,
        jnp.where(source_band < lat_index, lat_rows, lat_rows + 1),
    )
    gathered = jnp.take(candidates, pick_index, axis=1)
    species_count = gathered.shape[0]
    day_count = lat_rows // 2
    ranking = jnp.cumsum(day_flag) - 1
    wanted = (day_flag[None, :] == 1) & (
        ranking[None, :] == jnp.arange(day_count, dtype=jnp.int32)[:, None]
    )
    lit_slots = jnp.sum(wanted.astype(jnp.int32) * row_ids[None, :], axis=1)
    active = jnp.take(gathered, lit_slots, axis=1)
    reacted = react_cells(
        active.reshape(species_count, -1), reactants, products, rate_const
    ).reshape(active.shape)
    states = gathered.at[:, lit_slots].set(reacted)
    return states


def solution(mesh):
    in_specs = (P("spec", "lat", None), P("lat", None), P(), P(), P(), P(), P())
    out_specs = P(None, "lat", "spec")
    return jax.shard_map(
        on_device, mesh=mesh, in_specs=in_specs, out_specs=out_specs, check_vma=False
    )
```

profile of v0, /device:TPU:17, one launch (start us, length us, event | category | flops | bytes accessed | tf_op | source)
XLA Modules:
  0.0 144.8 jit_solution(2726070398159518174)
XLA Ops:
  0.0 1.6 %pad_maximum_fusion.8 = (f32[65,2,512]{2,1,0:T(2,128)S(1)}, f32[65,2,512]{2,1,0:T(2,128)S(1)}) fusion(f32[1,4,512]{2,1,0:T(4,128)} %bitcast.71, f32[64,4,512]{2,1,0:T(4,128)} %param.9), kind=kLoop, calls=%fused_computation.61 | loop fusion | flops 133120 | bytes 1064960 | tf_op jit(solution)/shard_map/concatenate | solution.py:72
  1.7 3.1 %collective-permute-start = (f32[65,2,512]{2,0,1:T(8,128)S(1)}, f32[65,2,512]{2,0,1:T(8,128)S(1)}, u32[]{:S(2)}, u32[]{:S(2)}) collective-permute-start(f32[65,2,512]{2,0,1:T(8,128)S(1)} %copy.66), channel_id=1, source_target_pairs={{1,0},{2,1},{3,2},{4,3},{5,4},{6,5},{7,6},{9,8},{10,9},{11,10},{12... | collective-permute-start | bytes 798728 | tf_op jit(solution)/shard_map/ppermute | solution.py:18
  4.9 2.3 %collective-permute-start.1 = (f32[65,2,512]{2,0,1:T(8,128)S(1)}, f32[65,2,512]{2,0,1:T(8,128)S(1)}, u32[]{:S(2)}, u32[]{:S(2)}) collective-permute-start(f32[65,2,512]{2,0,1:T(8,128)S(1)} %copy.68), channel_id=1, source_target_pairs={{0,1},{1,2},{2,3},{3,4},{4,5},{5,6},{6,7},{8,9},{9,10},{10,11},{11... | collective-permute-start | bytes 798728 | tf_op jit(solution)/shard_map/ppermute | solution.py:15
  7.8 10.1 %collective-permute-done = f32[65,2,512]{2,0,1:T(8,128)S(1)} collective-permute-done((f32[65,2,512]{2,0,1:T(8,128)S(1)}, f32[65,2,512]{2,0,1:T(8,128)S(1)}, u32[]{:S(2)}, u32[]{:S(2)}) %collective-permute-start) | collective-permute-done | bytes 266272 | tf_op jit(solution)/shard_map/ppermute | solution.py:18
  18.2 0.2 fusion.4
  18.4 0.5 collective-permute-done.1
  19.1 0.3 fusion.1
  19.6 0.7 minimum_multiply_fusion.1
  20.4 0.6 fusion.9
  21.0 0.2 fusion.19
  21.5 4.0 %collective-permute-start.2 = (f32[65,2,512]{2,0,1:T(8,128)S(1)}, f32[65,2,512]{2,0,1:T(8,128)S(1)}, u32[]{:S(2)}, u32[]{:S(2)}) collective-permute-start(f32[65,2,512]{2,0,1:T(8,128)S(1)} %copy.72), channel_id=1, source_target_pairs={{1,0},{2,1},{3,2},{4,3},{5,4},{6,5},{7,6},{9,8},{10,9},{11,10},{12... | collective-permute-start | bytes 798728 | tf_op jit(solution)/shard_map/ppermute | solution.py:18
  25.5 0.8 fusion.43
  30.4 2.0 %collective-permute-start.3 = (f32[65,2,512]{2,0,1:T(8,128)S(1)}, f32[65,2,512]{2,0,1:T(8,128)S(1)}, u32[]{:S(2)}, u32[]{:S(2)}) collective-permute-start(f32[65,2,512]{2,0,1:T(8,128)S(1)} %copy.74), channel_id=1, source_target_pairs={{0,1},{1,2},{2,3},{3,4},{4,5},{5,6},{6,7},{8,9},{9,10},{10,11},{11... | collective-permute-start | bytes 798728 | tf_op jit(solution)/shard_map/ppermute | solution.py:15
  32.7 0.2 fusion.5
  32.9 8.1 %collective-permute-done.3 = f32[65,2,512]{2,0,1:T(8,128)S(1)} collective-permute-done((f32[65,2,512]{2,0,1:T(8,128)S(1)}, f32[65,2,512]{2,0,1:T(8,128)S(1)}, u32[]{:S(2)}, u32[]{:S(2)}) %collective-permute-start.3) | collective-permute-done | bytes 266272 | tf_op jit(solution)/shard_map/ppermute | solution.py:15
  41.2 0.3 fusion.3
  41.7 0.7 minimum_multiply_fusion
  42.5 0.6 fusion.13
  43.1 0.2 fusion.18
  43.4 0.4 copy.78
  43.8 1.8 %reshape.360 = f32[4,1,32768]{2,1,0:T(1,128)} reshape(f32[512,4,64]{2,1,0:T(4,128)S(1)} %bitcast.65) | data formatting | bytes 1048576
  45.6 5.1 %all-to-all-start = ((f32[4,1,32768]{2,1,0:T(1,128)}), f32[4,1,32768]{2,1,0:T(1,128)S(1)}, u32[]{:S(2)}, u32[]{:S(2)}) async-start(f32[4,1,32768]{2,1,0:T(1,128)} %reshape.360), calls=%async_computation | async-start | bytes 1048576 | tf_op jit(solution)/shard_map/all_to_all | solution.py:75
  50.7 7.8 %all-to-all-done = f32[4,1,32768]{2,1,0:T(1,128)S(1)} async-done(((f32[4,1,32768]{2,1,0:T(1,128)}), f32[4,1,32768]{2,1,0:T(1,128)S(1)}, u32[]{:S(2)}, u32[]{:S(2)}) %all-to-all-start) | async-done | bytes 524320 | tf_op jit(solution)/shard_map/all_to_all | solution.py:75
  58.5 0.5 broadcast.400
  59.0 2.1 %reduce = f32[4,32768]{1,0:T(4,128)S(1)} reduce(f32[4,1,32768]{2,1,0:T(1,128)S(1)} %all-to-all-done, f32[]{:T(128)} %broadcast.400), dimensions={1}, to_apply=%all_to_all.13.reduce_sub_computation | reduce | bytes 1048580 | tf_op jit(solution)/shard_map/all_to_all | solution.py:75
  61.1 0.7 reshape.361
  61.9 0.3 copy.80
  62.2 1.9 %collective-permute-start.5 = (f32[256,1,128]{2,0,1:T(8,128)S(1)}, f32[256,1,128]{2,0,1:T(8,128)S(1)}, u32[]{:S(2)}, u32[]{:S(2)}) collective-permute-start(f32[256,1,128]{2,0,1:T(8,128)S(1)} %get-tuple-element.23), channel_id=1, source_target_pairs={{1,0},{2,1},{3,2},{4,3},{5,4},{6,5},{7,6},{9,8},{10,9},{11,10},{12... | collective-permute-start | bytes 393224 | tf_op jit(solution)/shard_map/ppermute | solution.py:26
  64.2 3.5 %collective-permute-start.4 = (f32[256,1,128]{2,0,1:T(8,128)S(1)}, f32[256,1,128]{2,0,1:T(8,128)S(1)}, u32[]{:S(2)}, u32[]{:S(2)}) collective-permute-start(f32[256,1,128]{2,0,1:T(8,128)S(1)} %get-tuple-element.22), channel_id=1, source_target_pairs={{0,1},{1,2},{2,3},{3,4},{4,5},{5,6},{6,7},{8,9},{9,10},{10,11},{11... | collective-permute-start | bytes 393224 | tf_op jit(solution)/shard_map/ppermute | solution.py:26
  68.0 2.8 %collective-permute-done.4 = f32[256,1,128]{2,0,1:T(8,128)S(1)} collective-permute-done((f32[256,1,128]{2,0,1:T(8,128)S(1)}, f32[256,1,128]{2,0,1:T(8,128)S(1)}, u32[]{:S(2)}, u32[]{:S(2)}) %collective-permute-start.4) | collective-permute-done | bytes 131104 | tf_op jit(solution)/shard_map/ppermute | solution.py:26
  70.9 0.6 gather_fusion
  71.6 0.6 gather_fusion.1
  72.4 3.5 %gather_fusion.3 = f32[1024,256]{1,0:T(8,128)S(1)} fusion(f32[256,256]{1,0:T(8,128)S(1)} %broadcast_select_fusion, s32[1024]{0:T(1024)S(1)} %fusion.39), kind=kCustom, calls=%fused_computation.1.clone | custom fusion | bytes 2101248 | tf_op jit(solution)/shard_map/jit(_take)/gather | solution.py:54
  75.9 3.5 %gather_fusion.2 = f32[1024,256]{1,0:T(8,128)S(1)} fusion(f32[256,256]{1,0:T(8,128)S(1)} %broadcast_select_fusion, s32[1024]{0:T(1024)S(1)} %fusion.38), kind=kCustom, calls=%fused_computation.clone | custom fusion | bytes 2101248 | tf_op jit(solution)/shard_map/jit(_take)/gather | solution.py:53
  79.4 1.7 %add_divide_fusion.1 = f32[1024,256]{1,0:T(8,128)} fusion(f32[1024,256]{1,0:T(8,128)S(1)} %gather_fusion.3, f32[1024,256]{1,0:T(8,128)S(1)} %gather_fusion.2, f32[1024]{0:T(1024)S(1)} %copy-done.2, pred[1024]{0:T(1024)(128)(4,1)S(1)} %get-tuple-element.28, pred[1024]{0:T(1024)(128)(4,1)S(1)} %get-tuple-element.29), kind=kLoop, calls=%fused_computation.48 | loop fusion | flops 1835008 | bytes 3151872 | tf_op jit(solution)/shard_map/div | solution.py:56
  81.1 6.6 %scatter_custom_fusion.2 = f32[256,256]{1,0:T(8,128)S(1)} fusion(s32[1024]{0:T(1024)S(1)} %bitcast.85, f32[1024,256]{1,0:T(8,128)} %add_divide_fusion.1, f32[]{:T(128)} %constant.99.clone.1), kind=kCustom, calls=%fused_computation.77 | custom fusion | flops 262144 | bytes 262656 | tf_op jit(solution)/shard_map/scatter-add | solution.py:59
  87.7 6.6 %scatter_custom_fusion.3 = f32[256,256]{1,0:T(8,128)S(1)} fusion(s32[1024]{0:T(1024)S(1)} %bitcast.81, f32[1024,256]{1,0:T(8,128)} %add_divide_fusion.1, f32[]{:T(128)} %constant.99.clone.1), kind=kCustom, calls=%fused_computation.75 | custom fusion | flops 262144 | bytes 262656 | tf_op jit(solution)/shard_map/scatter-add | solution.py:60
  94.3 6.6 %scatter_custom_fusion = f32[256,256]{1,0:T(8,128)S(1)} fusion(s32[1024]{0:T(1024)S(1)} %bitcast.89, f32[1024,256]{1,0:T(8,128)} %add_divide_fusion.1, f32[]{:T(128)} %constant.99.clone.1), kind=kCustom, calls=%fused_computation.81 | custom fusion | flops 262144 | bytes 262656 | tf_op jit(solution)/shard_map/scatter-add | solution.py:57
  100.9 6.8 %scatter_custom_fusion.1 = f32[256,256]{1,0:T(8,128)S(1)} fusion(s32[1024]{0:T(1024)S(1)} %bitcast.87, f32[1024,256]{1,0:T(8,128)} %add_divide_fusion.1, f32[]{:T(128)} %constant.99.clone.1), kind=kCustom, calls=%fused_computation.79 | custom fusion | flops 262144 | bytes 262656 | tf_op jit(solution)/shard_map/scatter-add | solution.py:58
  107.9 3.5 %gather_fusion.5 = f32[1024,256]{1,0:T(8,128)S(1)} fusion(f32[256,256]{1,0:T(8,128)S(1)} %subtract_add_fusion, s32[1024]{0:T(1024)S(1)} %fusion.39), kind=kCustom, calls=%fused_computation.3.clone | custom fusion | bytes 2101248 | tf_op jit(solution)/shard_map/jit(_take)/gather | solution.py:54
  111.3 3.5 %gather_fusion.4 = f32[1024,256]{1,0:T(8,128)S(1)} fusion(f32[256,256]{1,0:T(8,128)S(1)} %subtract_add_fusion, s32[1024]{0:T(1024)S(1)} %fusion.38), kind=kCustom, calls=%fused_computation.2.clone | custom fusion | bytes 2101248 | tf_op jit(solution)/shard_map/jit(_take)/gather | solution.py:53
  114.8 1.7 %add_divide_fusion = f32[1024,256]{1,0:T(8,128)} fusion(f32[1024,256]{1,0:T(8,128)S(1)} %gather_fusion.5, f32[1024,256]{1,0:T(8,128)S(1)} %gather_fusion.4, f32[1024]{0:T(1024)S(1)} %copy-done.2, pred[1024]{0:T(1024)(128)(4,1)S(1)} %get-tuple-element.28, pred[1024]{0:T(1024)(128)(4,1)S(1)} %get-tuple-element.29), kind=kLoop, calls=%fused_computation.47 | loop fusion | flops 1835008 | bytes 3151872 | tf_op jit(solution)/shard_map/div | solution.py:56
  116.5 6.6 %scatter_custom_fusion.6 = f32[256,256]{1,0:T(8,128)S(1)} fusion(s32[1024]{0:T(1024)S(1)} %bitcast.86, f32[1024,256]{1,0:T(8,128)} %add_divide_fusion, f32[]{:T(128)} %constant.99.clone.1), kind=kCustom, calls=%fused_computation.69 | custom fusion | flops 262144 | bytes 262656 | tf_op jit(solution)/shard_map/scatter-add | solution.py:59
  123.1 6.6 %scatter_custom_fusion.7 = f32[256,256]{1,0:T(8,128)S(1)} fusion(s32[1024]{0:T(1024)S(1)} %bitcast.82, f32[1024,256]{1,0:T(8,128)} %add_divide_fusion, f32[]{:T(128)} %constant.99.clone.1), kind=kCustom, calls=%fused_computation.67 | custom fusion | flops 262144 | bytes 262656 | tf_op jit(solution)/shard_map/scatter-add | solution.py:60
  129.7 6.6 %scatter_custom_fusion.4 = f32[256,256]{1,0:T(8,128)S(1)} fusion(s32[1024]{0:T(1024)S(1)} %bitcast.90, f32[1024,256]{1,0:T(8,128)} %add_divide_fusion, f32[]{:T(128)} %constant.99.clone.1), kind=kCustom, calls=%fused_computation.73 | custom fusion | flops 262144 | bytes 262656 | tf_op jit(solution)/shard_map/scatter-add | solution.py:57
  136.3 6.6 %scatter_custom_fusion.5 = f32[256,256]{1,0:T(8,128)S(1)} fusion(s32[1024]{0:T(1024)S(1)} %bitcast.88, f32[1024,256]{1,0:T(8,128)} %add_divide_fusion, f32[]{:T(128)} %constant.99.clone.1), kind=kCustom, calls=%fused_computation.71 | custom fusion | flops 262144 | bytes 262656 | tf_op jit(solution)/shard_map/scatter-add | solution.py:58
  143.0 0.6 scatter_fusion
  143.6 1.1 copy.84
  (56 shorter events, 3.2 us)
Async XLA Ops:
  0.0 7.2 %copy-start.5 = (s32[32]{0:T(128)S(1)}, s32[32]{0:T(128)}, u32[]{:S(2)}) copy-start(s32[32]{0:T(128)} %param.15) | copy-start | bytes 388
  0.0 7.2 %copy-start.6 = (s32[32]{0:T(128)S(1)}, s32[32]{0:T(128)}, u32[]{:S(2)}) copy-start(s32[32]{0:T(128)} %param.14) | copy-start | bytes 388
  0.0 7.4 %copy-start.3 = (s32[1024,2]{0,1:T(2,128)S(1)}, s32[1024,2]{0,1:T(2,128)}, u32[]{:S(2)}) copy-start(s32[1024,2]{0,1:T(2,128)} %param.12) | copy-start | bytes 24580
  1.6 16.5 %copy-start = (f32[64,4,512]{2,1,0:T(4,128)S(1)}, f32[64,4,512]{2,1,0:T(4,128)}, u32[]{:S(2)}) copy-start(f32[64,4,512]{2,1,0:T(4,128)} %param.9) | copy-start | bytes 1572868
  1.6 16.5 %copy-start.1 = (f32[4,512]{1,0:T(4,128)S(1)}, f32[4,512]{1,0:T(4,128)}, u32[]{:S(2)}) copy-start(f32[4,512]{1,0:T(4,128)} %param.10) | copy-start | bytes 24580
  1.7 16.2 %collective-permute-start = (f32[65,2,512]{2,0,1:T(8,128)S(1)}, f32[65,2,512]{2,0,1:T(8,128)S(1)}, u32[]{:S(2)}, u32[]{:S(2)}) collective-permute-start(f32[65,2,512]{2,0,1:T(8,128)S(1)} %copy.66), channel_id=1, source_target_pairs={{1,0},{2,1},{3,2},{4,3},{5,4},{6,5},{7,6},{9,8},{10,9},{11,10},{12... | collective-permute-start | bytes 798728 | tf_op jit(solution)/shard_map/ppermute | solution.py:18
  4.9 14.0 %collective-permute-start.1 = (f32[65,2,512]{2,0,1:T(8,128)S(1)}, f32[65,2,512]{2,0,1:T(8,128)S(1)}, u32[]{:S(2)}, u32[]{:S(2)}) collective-permute-start(f32[65,2,512]{2,0,1:T(8,128)S(1)} %copy.68), channel_id=1, source_target_pairs={{0,1},{1,2},{2,3},{3,4},{4,5},{5,6},{6,7},{8,9},{9,10},{10,11},{11... | collective-permute-start | bytes 798728 | tf_op jit(solution)/shard_map/ppermute | solution.py:15
  21.5 11.0 %collective-permute-start.2 = (f32[65,2,512]{2,0,1:T(8,128)S(1)}, f32[65,2,512]{2,0,1:T(8,128)S(1)}, u32[]{:S(2)}, u32[]{:S(2)}) collective-permute-start(f32[65,2,512]{2,0,1:T(8,128)S(1)} %copy.72), channel_id=1, source_target_pairs={{1,0},{2,1},{3,2},{4,3},{5,4},{6,5},{7,6},{9,8},{10,9},{11,10},{12... | collective-permute-start | bytes 798728 | tf_op jit(solution)/shard_map/ppermute | solution.py:18
  30.4 10.6 %collective-permute-start.3 = (f32[65,2,512]{2,0,1:T(8,128)S(1)}, f32[65,2,512]{2,0,1:T(8,128)S(1)}, u32[]{:S(2)}, u32[]{:S(2)}) collective-permute-start(f32[65,2,512]{2,0,1:T(8,128)S(1)} %copy.74), channel_id=1, source_target_pairs={{0,1},{1,2},{2,3},{3,4},{4,5},{5,6},{6,7},{8,9},{9,10},{10,11},{11... | collective-permute-start | bytes 798728 | tf_op jit(solution)/shard_map/ppermute | solution.py:15
  43.8 6.9 %copy-start.4 = (s32[1024,2]{0,1:T(2,128)S(1)}, s32[1024,2]{0,1:T(2,128)}, u32[]{:S(2)}) copy-start(s32[1024,2]{0,1:T(2,128)} %param.13) | copy-start | bytes 24580
  45.6 12.9 %all-to-all-start = ((f32[4,1,32768]{2,1,0:T(1,128)}), f32[4,1,32768]{2,1,0:T(1,128)S(1)}, u32[]{:S(2)}, u32[]{:S(2)}) async-start(f32[4,1,32768]{2,1,0:T(1,128)} %reshape.360), calls=%async_computation | async-start | bytes 1048576 | tf_op jit(solution)/shard_map/all_to_all | solution.py:75
  62.2 5.7 %collective-permute-start.5 = (f32[256,1,128]{2,0,1:T(8,128)S(1)}, f32[256,1,128]{2,0,1:T(8,128)S(1)}, u32[]{:S(2)}, u32[]{:S(2)}) collective-permute-start(f32[256,1,128]{2,0,1:T(8,128)S(1)} %get-tuple-element.23), channel_id=1, source_target_pairs={{1,0},{2,1},{3,2},{4,3},{5,4},{6,5},{7,6},{9,8},{10,9},{11,10},{12... | collective-permute-start | bytes 393224 | tf_op jit(solution)/shard_map/ppermute | solution.py:26
  64.2 6.6 %collective-permute-start.4 = (f32[256,1,128]{2,0,1:T(8,128)S(1)}, f32[256,1,128]{2,0,1:T(8,128)S(1)}, u32[]{:S(2)}, u32[]{:S(2)}) collective-permute-start(f32[256,1,128]{2,0,1:T(8,128)S(1)} %get-tuple-element.22), channel_id=1, source_target_pairs={{0,1},{1,2},{2,3},{3,4},{4,5},{5,6},{6,7},{8,9},{9,10},{10,11},{11... | collective-permute-start | bytes 393224 | tf_op jit(solution)/shard_map/ppermute | solution.py:26
  75.9 3.5 %copy-start.2 = (f32[1024]{0:T(1024)S(1)}, f32[1024]{0:T(1024)}, u32[]{:S(2)}) copy-start(f32[1024]{0:T(1024)} %param.11) | copy-start | bytes 12292
where the time goes:
time: 147 us; the launch traced here: 145 us
  other arithmetic  66.8 us (45%)
  waiting for transfers between devices  29.5 us (20%)
  local copies, waits for them, and re-layouts  22 us (15%)
  starting transfers between devices  22 us (15%)
  between operations  4.58 us (3%)
    scatter-add x2, other arithmetic, react_cells(): jax.ops.segment_sum(rates, products[:, 1], num_segments=species_count)  13.4 us
    scatter-add x2, other arithmetic, react_cells(): jax.ops.segment_sum(rates, products[:, 0], num_segments=species_count)  13.2 us
    scatter-add x2, other arithmetic, react_cells(): jax.ops.segment_sum(rates, reactants[:, 1], num_segments=species_count)  13.2 us
    scatter-add x2, other arithmetic, react_cells(): jax.ops.segment_sum(rates, reactants[:, 0], num_segments=species_count)  13.2 us
    ppermute x2, waiting for transfers between devices, padded_2(): lax.ppermute(lax.slice_in_dim(block, 0, width, axis=dim), axis, backward)  10.1 us
    ppermute x2, waiting for transfers between devices, padded_2(): lax.ppermute(lax.slice_in_dim(block, block.shape[dim] - width, None, axis...  8.58 us
    all_to_all x1, waiting for transfers between devices, on_device(): lax.all_to_all(values, 'spec', split_axis=2, concat_axis=0, tiled=True)  7.76 us
    ppermute x2, starting transfers between devices, padded_2(): lax.ppermute(lax.slice_in_dim(block, 0, width, axis=dim), axis, backward)  7.13 us
  transfers between devices with their start and end apart: 7, of which 6 were waited for; matrix products, arithmetic and copies ran while one was open for 2% of the time, Pallas kernels for 0%

commit v1 on v0

v1 whole, which is shorter than its diff:
```python
import functools

import jax
import jax.numpy as jnp
from jax import lax
from jax.experimental import pallas as pl
from jax.experimental.pallas import tpu as pltpu
from jax.sharding import Mesh
from jax.sharding import PartitionSpec as P

ADV_STEPS = 2
SUBSTEPS = 2
PAIR = 2
VMEM = pl.BlockSpec(memory_space=pltpu.VMEM)
SMEM = pl.BlockSpec(memory_space=pltpu.SMEM)


def params(mib):
    return pltpu.CompilerParams(vmem_limit_bytes=mib * 1024 * 1024)


def table_kernel(react_cols, react_rows, prod_rows, take_ref, net_ref):
    reactions, species = take_ref.shape[1:]
    lane = lax.broadcasted_iota(jnp.int32, (reactions, species), 1)
    for side in range(2):
        hit = react_cols[:, side : side + 1] == lane
        take_ref[side] = jnp.where(hit, 1.0, 0.0).astype(take_ref.dtype)
    line = lax.broadcasted_iota(jnp.int32, (species, reactions), 0)

    def ones(row):
        return jnp.where(row == line, 1.0, 0.0)

    net = ones(prod_rows[0:1, :]) + ones(prod_rows[1:2, :])
    net = net - ones(react_rows[0:1, :]) - ones(react_rows[1:2, :])
    net_ref[...] = net.astype(net_ref.dtype)


def mechanism_tables(reactants, products, species):
    reactions = reactants.shape[0]
    return pl.pallas_call(
        table_kernel,
        out_shape=(
            jax.ShapeDtypeStruct((2, reactions, species), jnp.bfloat16),
            jax.ShapeDtypeStruct((species, reactions), jnp.bfloat16),
        ),
        in_specs=[VMEM, VMEM, VMEM],
        out_specs=(VMEM, VMEM),
        compiler_params=params(16),
        cost_estimate=pl.CostEstimate(flops=20_000_000, bytes_accessed=2_000_000, transcendentals=0),
        name="tables",
    )(reactants, reactants.T, products.T)


def note_slots(slot_ref, day_ref, first_row, row_count, base_slot, rows, source_of, lit_of):
    total = slot_ref.shape[0]
    slot_count = source_of.shape[0]
    for step in range(row_count):
        row = first_row + step
        held = jnp.clip(row, 0, total - 1)
        slot = slot_ref[held] - base_slot

        @pl.when((row >= 0) & (row < total) & (slot >= 0) & (slot < slot_count))
        def _():
            at = jnp.clip(slot, 0, slot_count - 1)
            source_of[at] = step
            lit_of[at] = day_ref[held]


def places(lit_of, first, rows):
    lit_seen = jnp.int32(0)
    dark_seen = jnp.int32(rows // 2)
    found = []
    for step in range(rows):
        lit = lit_of[first + step]
        found.append(jnp.clip(jnp.where(lit == 1, lit_seen, dark_seen), 0, rows - 1))
        lit_seen = lit_seen + lit
        dark_seen = dark_seen + 1 - lit
    return found


def minmod(left, right):
    low = jnp.minimum(left, right)
    high = jnp.maximum(left, right)
    return jnp.maximum(low, 0.0) + jnp.minimum(high, 0.0)


def sweep(load, courant, store, first, count, valid):
    older = load(first - 2)
    old = load(first - 1)
    step_old = old - older
    here = load(first)
    step_here = here - old
    slope_old = minmod(step_here, step_old)
    flux_old = None
    for row in range(first, first + count + 1):
        following = load(row + 1)
        step_next = following - here
        slope_here = minmod(step_next, step_here)
        number = courant(row)
        up = jnp.maximum(number, 0.0)
        down = jnp.minimum(number, 0.0)
        up_half = up * (0.5 * (1.0 - number))
        down_half = down * (-0.5 * (1.0 + number))
        flux = (up * old + up_half * slope_old) + (down * here + down_half * slope_here)
        if flux_old is not None:
            store(row - 1, old - (flux - flux_old))
        old, here, step_here, slope_old, flux_old = here, following, step_next, slope_here, flux


def advect_kernel(
    own_ref, swap_ref, own_a, own_b, swap_a, swap_b, slot_ref, day_ref, out_ref,
    window, middle, advected, source_of, lit_of, order,
):
    species, rows, columns = own_ref.shape
    species = species - 1
    span = PAIR * rows
    band = lax.axis_index("band")
    side = lax.axis_index("pair")
    total = lax.axis_size("band") * span
    even = lax.rem(band, 2) == 0
    base_a = jnp.where(even, 2 * PAIR, 0)
    base_b = 2 * PAIR - base_a
    for ref, place in (
        (own_ref, PAIR + side),
        (swap_ref, PAIR + 1 - side),
        (own_a, base_a + side),
        (own_b, base_b + side),
        (swap_a, base_a + 1 - side),
        (swap_b, base_b + 1 - side),
    ):
        for row in range(rows):
            window[place * rows + row] = ref[:, row, :]

    reach = span // 2
    note_slots(slot_ref, day_ref, band * span - reach, span + 2 * reach, band * span, rows, source_of, lit_of)
    for half in range(PAIR):
        for slot, place in enumerate(places(lit_of, half * rows, rows)):
            order[half * rows + place] = source_of[half * rows + slot]

    first_row = band * span - span
    parts = out_ref.shape[0] // PAIR
    width = columns // parts

    def tile(part, carry):
        lanes = pl.ds(pl.multiple_of(part * width, width), width)

        def courant(row):
            at = first_row + row
            inside = (at >= 1) & (at <= total - 1)
            return jnp.where(inside, window[row, species : species + 1, lanes], 0.0)

        start = span - reach

        def store_middle(row, value):
            middle[row] = value

        def store_advected(row, value):
            advected[row - start] = value

        sweep(lambda row: window[row, 0:species, lanes], courant, store_middle, start - 2, span + 2 * reach + 4, None)
        sweep(lambda row: middle[row], courant, store_advected, start, span + 2 * reach, None)
        for half in range(PAIR):
            for place in range(rows):
                source = order[half * rows + place]
                out_ref[part * PAIR + half, place] = advected[source]
        return carry

    lax.fori_loop(0, parts, tile, 0)


def advect(own, swap, own_a, own_b, swap_a, swap_b, block_slot, daylit, parts):
    lines, rows, columns = own.shape
    species = lines - 1
    span = PAIR * rows
    width = columns // parts
    return pl.pallas_call(
        advect_kernel,
        out_shape=jax.ShapeDtypeStruct((parts * PAIR, rows, species, width), jnp.float32),
        in_specs=[VMEM] * 6 + [SMEM] * 2,
        out_specs=VMEM,
        scratch_shapes=[
            pltpu.VMEM((3 * span, lines, columns), jnp.float32),
            pltpu.VMEM((3 * span, species, width), jnp.float32),
            pltpu.VMEM((2 * span, species, width), jnp.float32),
            pltpu.SMEM((span,), jnp.int32),
            pltpu.SMEM((span,), jnp.int32),
            pltpu.SMEM((span,), jnp.int32),
        ],
        compiler_params=params(16),
        cost_estimate=pl.CostEstimate(flops=10_000_000, bytes_accessed=2_000_000, transcendentals=0),
        name="advect",
    )(own, swap, own_a, own_b, swap_a, swap_b, block_slot, daylit)


def split(value):
    high = value.astype(jnp.bfloat16)
    return high, (value - high.astype(jnp.float32)).astype(jnp.bfloat16)


def dot(left, right):
    return jnp.dot(left, right, preferred_element_type=jnp.float32)


def chemistry_kernel(cells_ref, take_ref, net_ref, const_ref, slot_ref, day_ref, out_ref, source_of, lit_of):
    chunks, rows, lines, width = cells_ref.shape
    species = chunks * lines
    reactions = const_ref.shape[0]
    group = lax.axis_index("band") * PAIR + lax.axis_index("pair")
    note_slots(slot_ref, day_ref, (group - 1) * rows, 3 * rows, group * rows, rows, source_of, lit_of)
    slots = places(lit_of, 0, rows)
    slot_of = [
        sum(jnp.where(place == at, slot, 0) for slot, place in enumerate(slots)) for at in range(rows)
    ]
    lit_rows = rows // 2

    def gathered(place):
        return cells_ref[:, place].reshape(species, width)

    for place in range(lit_rows, rows):
        out_ref[pl.ds(slot_of[place], species, stride=rows), :] = gathered(place)

    conc = jnp.concatenate([gathered(place) for place in range(lit_rows)], axis=1)
    block = min(256, reactions)
    for _ in range(SUBSTEPS):
        high, low = split(conc)
        change = jnp.zeros_like(conc)
        for at in range(0, reactions, block):
            one = dot(take_ref[0, at : at + block, :], high) + dot(take_ref[0, at : at + block, :], low)
            two = dot(take_ref[1, at : at + block, :], high) + dot(take_ref[1, at : at + block, :], low)
            encounter = one * two
            rates = const_ref[at : at + block, :] * encounter / (1.0 + jnp.abs(encounter))
            rate_high, rate_low = split(rates)
            net = net_ref[:, at : at + block]
            change = change + (dot(net, rate_high) + dot(net, rate_low))
        conc = conc + change
    for place in range(lit_rows):
        out_ref[pl.ds(slot_of[place], species, stride=rows), :] = conc[:, place * width : (place + 1) * width]


def chemistry(cells, take, net, rate_const, block_slot, daylit):
    chunks, rows, lines, width = cells.shape
    species = chunks * lines
    flat = pl.pallas_call(
        chemistry_kernel,
        out_shape=jax.ShapeDtypeStruct((species * rows, width), jnp.float32),
        in_specs=[VMEM] * 4 + [SMEM] * 2,
        out_specs=VMEM,
        scratch_shapes=[pltpu.SMEM((rows,), jnp.int32), pltpu.SMEM((rows,), jnp.int32)],
        compiler_params=params(24),
        name="chemistry",
    )(cells, take, net, rate_const[:, None], block_slot, daylit)
    return flat.reshape(species, rows, width)


def couples(count, first):
    pairs = []
    for low in range(first, count - 1, 2):
        pairs += [(low, low + 1), (low + 1, low)]
    return pairs


def on_device(concentration, courant, rate_const, reactants, products, daylit, block_slot):
    species_here = concentration.shape[0]
    half = species_here // PAIR
    parts = lax.axis_size("spec")
    bands = lax.axis_size("band")
    side = lax.axis_index("pair")
    flow = courant[None]

    def part(which):
        piece = lax.dynamic_slice_in_dim(concentration, which * half, half, axis=0)
        return jnp.concatenate([piece, flow], axis=0)

    own = part(side)
    other = part(1 - side)
    swap = lax.ppermute(other, "pair", couples(PAIR, 0))
    own_a = lax.ppermute(own, "band", couples(bands, 0))
    own_b = lax.ppermute(own, "band", couples(bands, 1))
    swap_a = lax.ppermute(swap, "band", couples(bands, 0))
    swap_b = lax.ppermute(swap, "band", couples(bands, 1))
    take, net = mechanism_tables(reactants, products, species_here * parts)
    chunks = advect(own, swap, own_a, own_b, swap_a, swap_b, block_slot, daylit, parts)
    cells = lax.all_to_all(chunks, ("spec", "pair"), split_axis=0, concat_axis=0, tiled=True)
    return chemistry(cells, take, net, rate_const, block_slot, daylit)


def solution(mesh):
    shape = (mesh.shape["spec"], mesh.shape["lat"] // PAIR, PAIR)
    inner = Mesh(mesh.devices.reshape(shape), ("spec", "band", "pair"))
    lat = ("band", "pair")
    in_specs = (P("spec", lat, None), P(lat, None), P(), P(), P(), P(), P())
    out_specs = P(None, lat, "spec")
    return jax.shard_map(on_device, mesh=inner, in_specs=in_specs, out_specs=out_specs, check_vma=False)
```

time: 147 us -> 41.3 us (0.28); the launches traced: 145 us -> 41 us
  other arithmetic: 66.8 us -> 0.14 us
  local copies, waits for them, and re-layouts: 22 us -> 2.46 us
  waiting for transfers between devices: 29.5 us -> 14.9 us
  Pallas kernels: 0 us -> 9.18 us
  starting transfers between devices: 22 us -> 14.2 us
  between operations: 4.58 us -> 0.09 us
    scatter-add x8 -> x0, other arithmetic: 53 us -> none  [the longest x2 13.4 us: react_cells(): jax.ops.segment_sum(rates, products[:, 1], num_segments=species_count)]
    gather x8 -> x0, local copies, waits for them, and re-layouts: 15.3 us -> none  [the longest x2 6.93 us: react_cells(): second_conc = jnp.take(conc, reactants[:, 1], axis=0)]
    ppermute x6 -> x5, waiting for transfers between devices: 21.7 us -> 9.13 us  [the longest x1 2.94 us: on_device(): swap = lax.ppermute(other, 'pair', couples(PAIR, 0))]
    ppermute x6 -> x5, starting transfers between devices: 16.9 us -> 7.69 us  [the longest x1 1.91 us: on_device(): own_b = lax.ppermute(own, 'band', couples(bands, 1))]
    pallas_call x0 -> x3, Pallas kernels: none -> 9.18 us  [the longest x1 4.69 us: chemistry(): pl.pallas_call(chemistry_kernel, out_shape=jax.ShapeDtypeStruct((species...]
    div x2 -> x0, other arithmetic: 3.43 us -> none  [react_cells(): rates = rate_const[:, None] * encounter / (1.0 + jnp.abs(encounter))]
    concatenate x7 -> x1, other arithmetic: 2.99 us -> 0.14 us  [part(): return jnp.concatenate([piece, flow], axis=0)]
    all_to_all x1 -> x0, other arithmetic: 2.14 us -> none  [on_device(): lax.all_to_all(values, 'spec', split_axis=2, concat_axis=0, tiled=True)]
  transfers between devices with their start and end apart: 7 -> 6, of which waited for: 6 -> 5; matrix products, arithmetic and copies ran while one was open for 2% -> 1% of each run, Pallas kernels for 0% -> 3%
where the time goes in v1:
time: 41.3 us; the launch traced here: 41 us
  waiting for transfers between devices  14.9 us (36%)
  starting transfers between devices  14.2 us (34%)
  Pallas kernels  9.18 us (22%)
  local copies, waits for them, and re-layouts  2.46 us (6%)
    all_to_all x1, starting transfers between devices, on_device(): lax.all_to_all(chunks, ('spec', 'pair'), split_axis=0, concat_axis=0, til...  6.52 us
    all_to_all x1, waiting for transfers between devices, on_device(): lax.all_to_all(chunks, ('spec', 'pair'), split_axis=0, concat_axis=0, til...  5.8 us
    pallas_call x1, Pallas kernels, chemistry(): pl.pallas_call(chemistry_kernel, out_shape=jax.ShapeDtypeStruct((species...  4.69 us
    pallas_call x1, Pallas kernels, advect(): pl.pallas_call(advect_kernel, out_shape=jax.ShapeDtypeStruct((parts * PAI...  3.19 us
    ppermute x1, waiting for transfers between devices, on_device(): swap = lax.ppermute(other, 'pair', couples(PAIR, 0))  2.94 us
    ppermute x1, waiting for transfers between devices, on_device(): swap_b = lax.ppermute(swap, 'band', couples(bands, 1))  2.9 us
    ppermute x1, waiting for transfers between devices, on_device(): swap_a = lax.ppermute(swap, 'band', couples(bands, 0))  2.69 us
    ppermute x1, starting transfers between devices, on_device(): own_b = lax.ppermute(own, 'band', couples(bands, 1))  1.91 us
  transfers between devices with their start and end apart: 6, of which 5 were waited for; matrix products, arithmetic and copies ran while one was open for 1% of the time, Pallas kernels for 3%

profile of v1, /device:TPU:17, one launch (start us, length us, event | category | flops | bytes accessed | tf_op | source)
XLA Modules:
  0.0 41.0 jit_solution(10210916676803934638)
XLA Ops:
  0.0 0.0 copy-start.4
  0.0 1.1 %constant_dynamic-slice_fusion = (f32[32,4,512]{2,1,0:T(4,128)S(1)}, f32[32,4,512]{2,1,0:T(4,128)S(1)}) fusion(f32[64,4,512]{2,1,0:T(4,128)} %param.7, s32[]{:T(128)S(6)} %select_n.7, s32[]{:T(128)S(6)} %select_n.6), kind=kLoop, calls=%fused_computation.2 | loop fusion | bytes 1048584 | tf_op jit(solution)/shard_map/dynamic_slice | solution.py:271
  1.1 0.0 copy-done.4
  1.1 0.1 pad_maximum_fusion
  1.2 0.0 copy-start.2
  1.2 0.0 copy-start.3
  1.3 1.3 %collective-permute-start = (f32[33,4,512]{2,1,0:T(4,128)S(1)}, f32[33,4,512]{2,1,0:T(4,128)S(1)}, u32[]{:S(2)}, u32[]{:S(2)}) collective-permute-start(f32[33,4,512]{2,1,0:T(4,128)S(1)} %get-tuple-element.11), channel_id=1, source_target_pairs={{0,1},{1,0},{2,3},{3,2},{4,5},{5,4},{6,7},{7,6},{8,9},{9,8},{10,11... | collective-permute-start | bytes 811016 | tf_op jit(solution)/shard_map/ppermute | solution.py:276
  2.5 1.3 %collective-permute-start.1 = (f32[33,4,512]{2,1,0:T(4,128)S(1)}, f32[33,4,512]{2,1,0:T(4,128)S(1)}, u32[]{:S(2)}, u32[]{:S(2)}) collective-permute-start(f32[33,4,512]{2,1,0:T(4,128)S(1)} %get-tuple-element.12.own_ref), channel_id=1, source_target_pairs={{0,2},{2,0},{4,6},{6,4},{1,3},{3,1},{5,7},{7,5},{8,10},{10,8},{12,... | collective-permute-start | bytes 811016 | tf_op jit(solution)/shard_map/ppermute | solution.py:277
  3.8 1.9 %collective-permute-start.2 = (f32[33,4,512]{2,1,0:T(4,128)S(1)}, f32[33,4,512]{2,1,0:T(4,128)S(1)}, u32[]{:S(2)}, u32[]{:S(2)}) collective-permute-start(f32[33,4,512]{2,1,0:T(4,128)S(1)} %get-tuple-element.12.own_ref), channel_id=1, source_target_pairs={{2,4},{4,2},{3,5},{5,3},{10,12},{12,10},{11,13},{13,11},{18,20},{2... | collective-permute-start | bytes 811016 | tf_op jit(solution)/shard_map/ppermute | solution.py:278
  5.8 2.9 %collective-permute-done.swap_ref = f32[33,4,512]{2,1,0:T(4,128)S(1)} collective-permute-done((f32[33,4,512]{2,1,0:T(4,128)S(1)}, f32[33,4,512]{2,1,0:T(4,128)S(1)}, u32[]{:S(2)}, u32[]{:S(2)}) %collective-permute-start) | collective-permute-done | bytes 270368 | tf_op jit(solution)/shard_map/ppermute | solution.py:276
  8.7 1.3 %collective-permute-start.3 = (f32[33,4,512]{2,1,0:T(4,128)S(1)}, f32[33,4,512]{2,1,0:T(4,128)S(1)}, u32[]{:S(2)}, u32[]{:S(2)}) collective-permute-start(f32[33,4,512]{2,1,0:T(4,128)S(1)} %collective-permute-done.swap_ref), channel_id=1, source_target_pairs={{0,2},{2,0},{4,6},{6,4},{1,3},{3,1},{5,7},{7,5},{8,10},{10,8},{12,... | collective-permute-start | bytes 811016 | tf_op jit(solution)/shard_map/ppermute | solution.py:279
  10.0 1.9 %collective-permute-start.4 = (f32[33,4,512]{2,1,0:T(4,128)S(1)}, f32[33,4,512]{2,1,0:T(4,128)S(1)}, u32[]{:S(2)}, u32[]{:S(2)}) collective-permute-start(f32[33,4,512]{2,1,0:T(4,128)S(1)} %collective-permute-done.swap_ref), channel_id=1, source_target_pairs={{2,4},{4,2},{3,5},{5,3},{10,12},{12,10},{11,13},{13,11},{18,20},{2... | collective-permute-start | bytes 811016 | tf_op jit(solution)/shard_map/ppermute | solution.py:280
  11.9 0.0 collective-permute-done.1.own_a
  11.9 0.6 %collective-permute-done.2.own_b = f32[33,4,512]{2,1,0:T(4,128)S(1)} collective-permute-done((f32[33,4,512]{2,1,0:T(4,128)S(1)}, f32[33,4,512]{2,1,0:T(4,128)S(1)}, u32[]{:S(2)}, u32[]{:S(2)}) %collective-permute-start.2) | collective-permute-done | bytes 270368 | tf_op jit(solution)/shard_map/ppermute | solution.py:278
  12.5 2.7 %collective-permute-done.3.swap_a = f32[33,4,512]{2,1,0:T(4,128)S(1)} collective-permute-done((f32[33,4,512]{2,1,0:T(4,128)S(1)}, f32[33,4,512]{2,1,0:T(4,128)S(1)}, u32[]{:S(2)}, u32[]{:S(2)}) %collective-permute-start.3) | collective-permute-done | bytes 270368 | tf_op jit(solution)/shard_map/ppermute | solution.py:279
  15.2 2.9 %collective-permute-done.4.swap_b = f32[33,4,512]{2,1,0:T(4,128)S(1)} collective-permute-done((f32[33,4,512]{2,1,0:T(4,128)S(1)}, f32[33,4,512]{2,1,0:T(4,128)S(1)}, u32[]{:S(2)}, u32[]{:S(2)}) %collective-permute-start.4) | collective-permute-done | bytes 270368 | tf_op jit(solution)/shard_map/ppermute | solution.py:280
  18.1 0.0 copy-done.2
  18.1 0.0 copy-done.3
  18.1 3.2 %advect.1 = f32[8,4,32,128]{3,2,1,0:T(8,128)} custom-call(f32[33,4,512]{2,1,0:T(4,128)S(1)} %get-tuple-element.12.own_ref, f32[33,4,512]{2,1,0:T(4,128)S(1)} %collective-permute-done.swap_ref, f32[33,4,512]{2,1,0:T(4,128)S(1)} %collective-permute-done.1.own_a, f32[33,4,512]{2,1,0:T(4,128)S(1)} %collective-permute-done.2.own_b, ...), custom_call_target="tpu_custom_call" | custom-call | flops 10000000 | bytes 2000000 | tf_op jit(solution)/shard_map/advect/pallas_call | solution.py:176
  21.3 0.0 copy-start
  21.3 6.5 %all-to-all-start = ((f32[8,4,32,128]{3,2,1,0:T(8,128)}), f32[8,4,32,128]{3,2,1,0:T(8,128)S(1)}, u32[]{:S(2)}, u32[]{:S(2)}) async-start(f32[8,4,32,128]{3,2,1,0:T(8,128)} %advect.1), calls=%async_computation | async-start | bytes 1048576 | tf_op jit(solution)/shard_map/all_to_all | solution.py:283
  27.8 0.0 copy-done
  27.8 0.0 copy-start.5
  27.8 0.2 copy.9.react_cols
  28.0 0.5 %copy-done.5 = f32[1024]{0:T(1024)S(1)} copy-done((f32[1024]{0:T(1024)S(1)}, f32[1024]{0:T(1024)}, u32[]{:S(2)}) %copy-start.5) | copy-done | bytes 4120
  28.5 0.0 copy-start.1
  28.5 0.2 copy.10.const_ref
  28.7 0.5 %copy-done.1 = s32[1024,2]{0,1:T(2,128)S(1)} copy-done((s32[1024,2]{0,1:T(2,128)S(1)}, s32[1024,2]{0,1:T(2,128)}, u32[]{:S(2)}) %copy-start.1) | copy-done | bytes 8216
  29.2 1.3 %tables.1 = (bf16[2,1024,256]{2,1,0:T(8,128)(2,1)S(1)}, bf16[256,1024]{1,0:T(8,128)(2,1)S(1)}) custom-call(s32[1024,2]{1,0:T(8,128)S(1)} %copy.9.react_cols, s32[2,1024]{1,0:T(2,128)S(1)} %bitcast.5, s32[2,1024]{1,0:T(2,128)S(1)} %bitcast.6), custom_call_target="tpu_custom_call" | custom-call | flops 20000000 | bytes 2000000 | tf_op jit(solution)/shard_map/tables/pallas_call | solution.py:40
  30.5 5.8 %all-to-all-done.cells_ref = f32[8,4,32,128]{3,2,1,0:T(8,128)S(1)} async-done(((f32[8,4,32,128]{3,2,1,0:T(8,128)}), f32[8,4,32,128]{3,2,1,0:T(8,128)S(1)}, u32[]{:S(2)}, u32[]{:S(2)}) %all-to-all-start) | async-done | bytes 524320 | tf_op jit(solution)/shard_map/all_to_all | solution.py:283
  36.3 4.7 %chemistry.1 = f32[1024,128]{1,0:T(8,128)} custom-call(f32[8,4,32,128]{3,2,1,0:T(8,128)S(1)} %all-to-all-done.cells_ref, bf16[2,1024,256]{2,1,0:T(8,128)(2,1)S(1)} %get-tuple-element.7.take_ref, bf16[256,1024]{1,0:T(8,128)(2,1)S(1)} %get-tuple-element.8.net_ref, f32[1024,1]{1,0:T(8,128)S(1)} %copy.10.const_ref, s32[32]{0:T(128)S(1)} %copy-done.2, ...), custom_call_target="tpu_custom_call" | custom-call | tf_op jit(solution)/shard_map/chemistry/pallas_call | solution.py:243
Async XLA Ops:
  0.0 1.1 %copy-start.4 = (f32[4,512]{1,0:T(4,128)S(1)}, f32[4,512]{1,0:T(4,128)}, u32[]{:S(2)}) copy-start(f32[4,512]{1,0:T(4,128)} %param.8) | copy-start | bytes 24580
  1.2 16.9 %copy-start.2 = (s32[32]{0:T(128)S(1)}, s32[32]{0:T(128)}, u32[]{:S(2)}) copy-start(s32[32]{0:T(128)} %slot_ref.3) | copy-start | bytes 388
  1.2 16.9 %copy-start.3 = (s32[32]{0:T(128)S(1)}, s32[32]{0:T(128)}, u32[]{:S(2)}) copy-start(s32[32]{0:T(128)} %day_ref.3) | copy-start | bytes 388
  1.3 7.4 %collective-permute-start = (f32[33,4,512]{2,1,0:T(4,128)S(1)}, f32[33,4,512]{2,1,0:T(4,128)S(1)}, u32[]{:S(2)}, u32[]{:S(2)}) collective-permute-start(f32[33,4,512]{2,1,0:T(4,128)S(1)} %get-tuple-element.11), channel_id=1, source_target_pairs={{0,1},{1,0},{2,3},{3,2},{4,5},{5,4},{6,7},{7,6},{8,9},{9,8},{10,11... | collective-permute-start | bytes 811016 | tf_op jit(solution)/shard_map/ppermute | solution.py:276
  2.5 9.4 %collective-permute-start.1 = (f32[33,4,512]{2,1,0:T(4,128)S(1)}, f32[33,4,512]{2,1,0:T(4,128)S(1)}, u32[]{:S(2)}, u32[]{:S(2)}) collective-permute-start(f32[33,4,512]{2,1,0:T(4,128)S(1)} %get-tuple-element.12.own_ref), channel_id=1, source_target_pairs={{0,2},{2,0},{4,6},{6,4},{1,3},{3,1},{5,7},{7,5},{8,10},{10,8},{12,... | collective-permute-start | bytes 811016 | tf_op jit(solution)/shard_map/ppermute | solution.py:277
  3.8 8.7 %collective-permute-start.2 = (f32[33,4,512]{2,1,0:T(4,128)S(1)}, f32[33,4,512]{2,1,0:T(4,128)S(1)}, u32[]{:S(2)}, u32[]{:S(2)}) collective-permute-start(f32[33,4,512]{2,1,0:T(4,128)S(1)} %get-tuple-element.12.own_ref), channel_id=1, source_target_pairs={{2,4},{4,2},{3,5},{5,3},{10,12},{12,10},{11,13},{13,11},{18,20},{2... | collective-permute-start | bytes 811016 | tf_op jit(solution)/shard_map/ppermute | solution.py:278
  8.7 6.5 %collective-permute-start.3 = (f32[33,4,512]{2,1,0:T(4,128)S(1)}, f32[33,4,512]{2,1,0:T(4,128)S(1)}, u32[]{:S(2)}, u32[]{:S(2)}) collective-permute-start(f32[33,4,512]{2,1,0:T(4,128)S(1)} %collective-permute-done.swap_ref), channel_id=1, source_target_pairs={{0,2},{2,0},{4,6},{6,4},{1,3},{3,1},{5,7},{7,5},{8,10},{10,8},{12,... | collective-permute-start | bytes 811016 | tf_op jit(solution)/shard_map/ppermute | solution.py:279
  10.0 8.1 %collective-permute-start.4 = (f32[33,4,512]{2,1,0:T(4,128)S(1)}, f32[33,4,512]{2,1,0:T(4,128)S(1)}, u32[]{:S(2)}, u32[]{:S(2)}) collective-permute-start(f32[33,4,512]{2,1,0:T(4,128)S(1)} %collective-permute-done.swap_ref), channel_id=1, source_target_pairs={{2,4},{4,2},{3,5},{5,3},{10,12},{12,10},{11,13},{13,11},{18,20},{2... | collective-permute-start | bytes 811016 | tf_op jit(solution)/shard_map/ppermute | solution.py:280
  21.3 6.5 %copy-start = (s32[1024,2]{0,1:T(2,128)S(1)}, s32[1024,2]{0,1:T(2,128)}, u32[]{:S(2)}) copy-start(s32[1024,2]{0,1:T(2,128)} %param.10) | copy-start | bytes 24580
  21.3 15.0 %all-to-all-start = ((f32[8,4,32,128]{3,2,1,0:T(8,128)}), f32[8,4,32,128]{3,2,1,0:T(8,128)S(1)}, u32[]{:S(2)}, u32[]{:S(2)}) async-start(f32[8,4,32,128]{3,2,1,0:T(8,128)} %advect.1), calls=%async_computation | async-start | bytes 1048576 | tf_op jit(solution)/shard_map/all_to_all | solution.py:283
  27.8 0.7 %copy-start.5 = (f32[1024]{0:T(1024)S(1)}, f32[1024]{0:T(1024)}, u32[]{:S(2)}) copy-start(f32[1024]{0:T(1024)} %param.9) | copy-start | bytes 12292
  28.5 0.7 %copy-start.1 = (s32[1024,2]{0,1:T(2,128)S(1)}, s32[1024,2]{0,1:T(2,128)}, u32[]{:S(2)}) copy-start(s32[1024,2]{0,1:T(2,128)} %param.11) | copy-start | bytes 24580
